TPU v7x, 512 devices: a whole 4x4x16 slice. The times are simulated.
512 devices in a mesh: prow: 16 (over y, z_hi, core), pcol: 32 (over x, z_lo).
Axes of the slice: x: 4, y: 4, z: 16 (z_hi: 2, z_lo: 8; z = z_hi * 8 + z_lo), core: 2. Of those that a mesh axis runs over, the one named last changes fastest.
Arguments:
- tiles: bfloat16 [16, 32, 16, 256, 256], P('prow', 'pcol'), may hold values from -6 to 6
- tile_ids: int32 [16, 32, 16], P('prow', 'pcol'), may hold values from 0 to 127, as said below
- counts: int32 [16, 32], P('prow', 'pcol'), may hold values from 1 to 16, as said below
- pivots: int32 [256], replicated, may hold values from 0 to 65535, as said below
- l_inverse: bfloat16 [256, 256], P(None, 'pcol'), may hold values from -1 to 1, as said below
- u_inverse: bfloat16 [256, 256], P('prow'), may hold values from -0.125 to 0.5, as said below
Outputs:
- factored: bfloat16 [16, 32, 16, 256, 256], P('prow', 'pcol')
Inputs may be any that keep to these rules, and one draw needn't show every extreme that they name: Live slot s of device (p, q) holds local tile row tile_ids[p, q, s] // 8 and local tile column tile_ids[p, q, s] % 8; live codes of one device are distinct, padded slots hold arbitrary codes. Let R be the tile rows I >= 1 with tile (I, 0) held and C the tile columns J >= 1 with tile (0, J) held. Tile (0, 0) is held; on each prow index R takes the last one to 3 local tile rows, on each pcol index C takes the last one to 3 local tile columns, and both most counts are reached on some index. Every tile whose row is 0 or in R and whose column is 0 or in C is held; no other held tile lies in tile row 0, a tile row of R, or tile column 0. `counts`: some device has 16 live slots. Row r of tile row 0 and row pivots[r] change places; pivots[r] is r or a row of a tile row of R, and the values that differ from their r are distinct. `l_inverse`: lower triangular with unit diagonal. `u_inverse`: upper triangular with a positive diagonal.
All inputs are finite; a program needn't handle non-finite values.
Results may differ from a plain program's by a relative error of at most 0.0056.
Values may be sent and summed in bfloat16 or wider, within the bound.
No kernel may reach another device: no remote copies, remote signals or barrier semaphores. Data moves between devices by JAX's collectives and lax.ppermute only.
A program may use at most 64 MiB of HBM per device.

v0:
```python
import jax
import jax.numpy as jnp
from jax import lax
from jax.sharding import Mesh
from jax.sharding import PartitionSpec as P

TILE_SIDE = 256
LOCAL_ROWS = 16
TILE_SLOTS = 16
LOWER_MOST = 3
UPPER_MOST = 3
HALF_WORK = 4
PCOL = ("pcol_0", "pcol_1")


def laid_out(parts, dim):
    parts = jnp.moveaxis(parts, 0, dim)
    lengths = parts.shape
    return parts.reshape(*lengths[:dim], lengths[dim] * lengths[dim + 1], *lengths[dim + 2 :])


def from_everyone(shard, axis):
    devices = lax.axis_size(axis)
    return lax.all_to_all(
        jnp.broadcast_to(shard[None], (devices, *shard.shape)), axis, 0, 0, tiled=True
    )


def gather_directly(shard, axis, dim):
    return laid_out(from_everyone(shard, axis), dim)


def spread(shard, axes, root):
    shard = jnp.where(lax.axis_index(axes) == root, shard, jnp.zeros_like(shard))
    for axis in axes:
        shard = lax.psum(shard, axis)
    return shard


def from_partner(block, axis, bit):
    count = lax.axis_size(axis)
    route = []
    for low in range(count):
        high = low | 1 << bit
        if high != low and high < count:
            route += [(low, high), (high, low)]
    return lax.ppermute(block, axis, route)


def pick_rows(tile, rows):
    return tile[rows]


def body(tiles, tile_ids, counts, pivots, l_inverse, u_inverse):
    row_count = lax.axis_size("prow")
    col_count = lax.axis_size(PCOL)
    my_row = lax.axis_index("prow")
    my_col = lax.axis_index(PCOL)
    grid_cols = LOCAL_ROWS * row_count // col_count
    total_rows = LOCAL_ROWS * row_count * TILE_SIDE
    local = tiles[0, 0]
    codes = tile_ids[0, 0]
    slot_range = jnp.arange(TILE_SLOTS, dtype=jnp.int32)
    alive = slot_range < counts[0, 0]
    loc_row = codes // grid_cols
    loc_col = codes % grid_cols
    glob_row = my_row + row_count * loc_row
    glob_col = my_col + col_count * loc_col
    col_range = jnp.arange(grid_cols, dtype=jnp.int32)
    upper_inv = lax.all_gather(u_inverse, "prow", axis=0, tiled=True)
    lower_inv = gather_directly(l_inverse, PCOL, 1)
    source_tile = pivots // TILE_SIDE
    source_row = pivots % TILE_SIDE
    gathered = local[:, source_row, :]
    owned = (source_tile[None, :] == glob_row[:, None]) & alive[:, None]
    contrib = jnp.where(owned[:, :, None], gathered, jnp.zeros_like(gathered))
    col_hot = ((loc_col[:, None] == col_range[None, :]) & alive[:, None]).astype(jnp.bfloat16)
    top_flag = (glob_row == 0).astype(jnp.bfloat16)
    top_hot = col_hot * top_flag[:, None]
    flag_part = jnp.sum(
        top_hot.astype(jnp.float32) * (glob_col >= 1).astype(jnp.float32)[:, None], axis=0
    )
    list_size = UPPER_MOST + 1
    rows_used = (glob_row == 0) | jnp.any(owned, axis=1)
    col_mask = jnp.any(
        (loc_col[:, None] == col_range[None, :]) & (alive & rows_used)[:, None], axis=0
    )
    listed = jnp.argsort(jnp.where(col_mask, 0, 1), stable=True)[:list_size]
    list_valid = col_mask[listed]
    list_hot = (
        (loc_col[:, None] == listed[None, :]) & list_valid[None, :] & alive[:, None]
    ).astype(jnp.bfloat16)
    new_part = jnp.einsum("sk,srb->krb", list_hot, contrib, preferred_element_type=jnp.float32)
    old_part = jnp.einsum(
        "sk,srb->krb", list_hot * top_flag[:, None], local, preferred_element_type=jnp.float32
    )
    id_part = jnp.where(list_valid & (my_row == 0), listed + 1, 0).astype(jnp.float32)
    new_sum, old_sum, flag_sum, id_sum = (
        lax.psum(new_part.astype(jnp.bfloat16), "prow").astype(jnp.float32),
        lax.psum(old_part.astype(jnp.bfloat16), "prow").astype(jnp.float32),
        lax.psum(flag_part.astype(jnp.bfloat16), "prow").astype(jnp.float32),
        lax.psum(id_part.astype(jnp.bfloat16), "prow").astype(jnp.float32),
    )
    list_ids = (id_sum + 0.5).astype(jnp.int32) - 1
    back_hot = ((list_ids[:, None] == col_range[None, :]) & (id_sum > 0.5)[:, None]).astype(
        jnp.bfloat16
    )
    new_top = jnp.einsum(
        "kj,krb->jrb", back_hot, new_sum.astype(jnp.bfloat16), preferred_element_type=jnp.float32
    ).astype(jnp.bfloat16)
    old_top = jnp.einsum(
        "kj,krb->jrb", back_hot, old_sum.astype(jnp.bfloat16), preferred_element_type=jnp.float32
    ).astype(jnp.bfloat16)
    anchor_top = (
        jnp.full((total_rows,), -1, jnp.int32)
        .at[pivots]
        .set(jnp.arange(TILE_SIDE, dtype=jnp.int32))
    )
    row_index = glob_row[:, None] * TILE_SIDE + jnp.arange(TILE_SIDE, dtype=jnp.int32)[None, :]
    anchor = anchor_top[row_index]
    moved = (anchor >= 0) & (glob_row >= 1)[:, None]
    from_top = jax.vmap(pick_rows)(old_top[loc_col], jnp.maximum(anchor, 0))
    swapped = jnp.where(moved[:, :, None], from_top, local)
    primed = jnp.where((glob_row == 0)[:, None, None], new_top[loc_col], swapped)
    panel_mask = alive & (glob_col == 0) & (glob_row >= 1)
    panel_slots = jnp.argsort(jnp.where(panel_mask, 0, 1), stable=True)[:LOWER_MOST]
    panel_valid = panel_mask[panel_slots]
    lower_full = jnp.einsum(
        "kab,bc->kac", primed[panel_slots], upper_inv, preferred_element_type=jnp.float32
    )
    lower_list = jnp.where(panel_valid[:, None, None], lower_full, 0.0).astype(jnp.bfloat16)
    lower_rows = jnp.where(panel_valid, loc_row[panel_slots], -1)
    got_list, got_rows = (spread(lower_list, PCOL, 0), spread(lower_rows, PCOL, 0))
    row_match = got_rows[None, :] == loc_row[:, None]
    lower_pick = jnp.sum(
        jnp.where(row_match, jnp.arange(LOWER_MOST, dtype=jnp.int32)[None, :], 0), axis=1
    )
    lower_present = jnp.any(row_match, axis=1)
    column_flags = flag_sum > 0.5
    column_order = jnp.argsort(jnp.where(column_flags, 0, 1), stable=True)[:UPPER_MOST]
    upper_valid = column_flags[column_order]
    upper_full = jnp.einsum(
        "ab,kbc->kac", lower_inv, new_top[column_order], preferred_element_type=jnp.float32
    )
    upper_list = jnp.where(upper_valid[:, None, None], upper_full, 0.0).astype(jnp.bfloat16)
    upper_ids = jnp.where(upper_valid, column_order, -1)
    col_match = upper_ids[None, :] == loc_col[:, None]
    upper_pick = jnp.sum(
        jnp.where(col_match, jnp.arange(UPPER_MOST, dtype=jnp.int32)[None, :], 0), axis=1
    )
    upper_present = jnp.any(col_match, axis=1)
    result = jnp.where(alive[:, None, None], primed, jnp.zeros_like(primed))
    upper_mask = alive & (glob_row == 0) & (glob_col >= 1)
    result = jnp.where(upper_mask[:, None, None], upper_list[upper_pick], result)
    result = result.at[panel_slots].set(
        jnp.where(panel_valid[:, None, None], lower_list, result[panel_slots])
    )
    needs = alive & (glob_row >= 1) & (glob_col >= 1) & lower_present & upper_present
    order = jnp.argsort(jnp.where(needs, 0, 1), stable=True)
    needed = jnp.sum(needs.astype(jnp.int32))

    def trailing(current, lower_tile, upper_index):
        product = jnp.dot(lower_tile, upper_list[upper_index], preferred_element_type=jnp.float32)
        return (current.astype(jnp.float32) - product).astype(jnp.bfloat16)

    half_index = jnp.arange(HALF_WORK, dtype=jnp.int32)
    odd_slots = order[2 * half_index + 1]
    sent_count = needed // 2
    partner_bit = row_count.bit_length() - 2
    got_tiles, got_lower, got_pick, got_count = from_partner(
        (primed[odd_slots], got_list[lower_pick[odd_slots]], upper_pick[odd_slots], sent_count),
        "prow",
        partner_bit,
    )

    def remote_step(position, held):
        value = trailing(got_tiles[position], got_lower[position], got_pick[position])
        return held.at[position].set(value)

    finished = lax.fori_loop(0, got_count, remote_step, jnp.zeros_like(got_tiles))
    returned = from_partner(finished, "prow", partner_bit)

    def even_step(position, held):
        slot = order[2 * position]
        value = trailing(primed[slot], got_list[lower_pick[slot]], upper_pick[slot])
        return held.at[slot].set(value)

    result = lax.fori_loop(0, (needed + 1) // 2, even_step, result)
    sent_live = half_index < sent_count
    result = result.at[odd_slots].set(
        jnp.where(sent_live[:, None, None], returned, result[odd_slots])
    )
    return result[None, None]


def solution(mesh):
    torus = Mesh(mesh.devices.reshape(mesh.shape["prow"], 4, 8), ("prow", "pcol_0", "pcol_1"))
    placed = (
        P("prow", PCOL, None, None, None),
        P("prow", PCOL, None),
        P("prow", PCOL),
        P(),
        P(None, PCOL),
        P("prow", None),
    )
    return jax.shard_map(
        body,
        mesh=torus,
        in_specs=placed,
        out_specs=P("prow", PCOL, None, None, None),
        check_vma=False,
    )
```

profile of v0, /device:TPU:484, one launch (start us, length us, event | category | flops | bytes accessed | tf_op | source)
XLA Modules:
  0.0 684.1 jit_solution(12001899202512432619)
XLA Ops:
  7.9 12.5 %all-to-all-start = ((bf16[32,256,8]{1,2,0:T(8,128)(2,1)}), bf16[32,256,8]{1,2,0:T(8,128)(2,1)S(1)}, u32[]{:S(2)}, u32[]{:S(2)}) async-start(bf16[32,256,8]{1,2,0:T(8,128)(2,1)} %broadcast_in_dim.201), calls=%async_computation | async-start | bytes 262144 | tf_op jit(solution)/shard_map/all_to_all | solution.py:24
  25.0 4.1 copy.83
  29.1 3.8 gather_fusion.2
  32.9 2.1 convolution_convert_fusion.2
  35.0 2.2 fusion.20
  37.4 61.9 %all-reduce = (bf16[4]{0:T(256)(128)(2,1)S(1)}, bf16[8]{0:T(256)(128)(2,1)S(1)}) all-reduce(bf16[4]{0:T(256)(128)(2,1)S(1)} %get-tuple-element.249, bf16[8]{0:T(256)(128)(2,1)S(1)} %multiply_reduce_fusion), channel_id=1, replica_groups=mesh['prow'=16,'pcol_0'=4,'pcol_1'=8] {'prow'}, use_global_device_ids=true, to_apply=%region_6.7 | all-reduce | flops 12 | bytes 48 | tf_op jit(solution)/shard_map/psum | solution.py:102
  103.7 6.4 psum.60
  110.2 9.6 %psum.61 = s32[3]{0:T(128)S(1)} all-reduce(s32[3]{0:T(128)S(1)} %psum.60), channel_id=1, replica_groups=mesh['prow'=16,'pcol_0'=4,'pcol_1'=8] {'pcol_1'}, use_global_device_ids=true, to_apply=%region_14.15 | all-reduce | flops 3 | bytes 24 | tf_op jit(solution)/shard_map/psum | solution.py:36
  122.1 23.0 %gather_fusion.6 = s32[4096]{0:T(1024)S(1)} fusion(s32[65536]{0:T(1024)S(1)} %scatter_custom_fusion, s32[4096]{0:T(1024)S(1)} %broadcast_clamp_fusion), kind=kCustom, calls=%fused_computation.6 | custom fusion | bytes 49152 | tf_op jit(solution)/shard_map/gather | solution.py:120
  145.5 46.9 %all_gather.3 = bf16[256,256]{1,0:T(8,128)(2,1)S(1)} all-gather(bf16[16,256]{1,0:T(8,128)(2,1)S(1)} %copy-done.9), channel_id=1, replica_groups=mesh['prow'=16,'pcol_0'=4,'pcol_1'=8] {'prow'}, dimensions={0}, use_global_device_ids=true | all-gather | bytes 139264 | tf_op jit(solution)/shard_map/all_gather | solution.py:70
  192.5 108.3 %all-reduce.10.cloned.1.call-done = (bf16[4,256,256]{2,0,1:T(4,128)(2,1)}, bf16[4,256,256]{2,0,1:T(4,128)(2,1)}) async-done(((bf16[4,256,256]{2,0,1:T(4,128)(2,1)}, bf16[4,256,256]{2,0,1:T(4,128)(2,1)}), (bf16[4,256,256]{2,0,1:T(4,128)(2,1)}, bf16[4,256,256]{2,0,1:T(4,128)(2,1)})) %all-reduce.10.cloned.1.call-update) | async-done | bytes 1048592 | tf_op jit(solution)/shard_map/psum | solution.py:99
  304.9 2.0 gather_fusion.5
  309.1 40.7 %gather_fusion.18 = bf16[4096,256]{1,0:T(8,128)(2,1)} fusion(bf16[16,256,256]{2,1,0:T(8,128)(2,1)S(1)} %gather_fusion.7, s32[4096]{0:T(1024)S(1)} %bitcast.154), kind=kCustom, calls=%fused_computation.18 | custom fusion | bytes 4227072 | tf_op jit(solution)/shard_map/vmap()/gather | solution.py:51
  349.8 2.0 gather_fusion.4
  351.8 16.1 %copy_select_fusion = (bf16[16,256,256]{2,0,1:T(8,128)(2,1)}, bf16[16,256,256]{2,0,1:T(8,128)(2,1)S(1)}) fusion(bf16[16,256,256]{2,1,0:T(8,128)(2,1)} %gather_fusion.4, pred[16]{0:T(512)(128)(4,1)S(1)} %iota_compare_fusion.3, pred[16]{0:T(512)(128)(4,1)S(1)} %copy-done.13, bf16[1,1,16,256,256]{4,3,2,1,0:T(8,128)(2,1)S(1)} %copy-done.1, ...), kind=kLoop, calls=%fused_computation.46 | loop fusion | flops 4194304 | bytes 12587056 | tf_op jit(solution)/shard_map/jit(_where)/select_n | solution.py:154
  370.0 2.3 copy.61
  376.2 68.7 %all-reduce.6.cloned.1.call-done = bf16[3,256,256]{2,1,0:T(8,128)(2,1)} async-done(((bf16[3,256,256]{2,1,0:T(8,128)(2,1)}), bf16[3,256,256]{2,1,0:T(8,128)(2,1)}) %all-reduce.6.cloned.1.call-update) | async-done | bytes 393232 | tf_op jit(solution)/shard_map/psum | solution.py:36
  445.6 3.0 gather_fusion.13
  448.5 4.9 collective-permute-start.1
  453.5 117.4 %all-reduce.8.cloned.1.call-done = bf16[3,256,256]{2,1,0:T(8,128)(2,1)} async-done(((bf16[3,256,256]{2,1,0:T(8,128)(2,1)}), bf16[3,256,256]{2,1,0:T(8,128)(2,1)}) %all-reduce.8.cloned.1.call-update) | async-done | bytes 393232 | tf_op jit(solution)/shard_map/psum | solution.py:36
  570.8 2.4 gather_fusion.15
  573.2 4.9 collective-permute-start.2
  581.0 4.1 collective-permute-start
  585.8 4.5 collective-permute-start.3
  593.6 6.5 while.23
  597.6 1.8 fusion.73
  600.1 21.9 %collective-permute-start.4 = (bf16[4,256,256]{2,1,0:T(8,128)(2,1)S(1)}, bf16[4,256,256]{2,1,0:T(8,128)(2,1)}, u32[]{:S(2)}, u32[]{:S(2)}) collective-permute-start(bf16[4,256,256]{2,1,0:T(8,128)(2,1)S(1)} %get-tuple-element.124), channel_id=1, source_target_pairs={{0,256},{256,0},{32,288},{288,32},{64,320},{320,64},{96,352},{352,... | collective-permute-start | bytes 1572872 | tf_op jit(solution)/shard_map/ppermute | solution.py:47
  622.0 50.8 %while.22 = (s32[]{:T(128)}, bf16[16,256,256]{2,1,0:T(8,128)(2,1)S(1)}, s32[]{:T(128)}, s32[16]{0:T(128)S(1)}, bf16[16,256,256]{2,1,0:T(8,128)(2,1)}, /*index=5*...) while((s32[]{:T(128)}, ...), condition=%wide.region_24.25_spmd, body=%wide.region_22.24_spmd.sunk | while | flops 33816608 | bytes 656746 | solution.py:188
  630.4 1.8 fusion.70
  640.5 1.8 fusion.70
  650.7 1.8 fusion.70
  671.0 1.8 fusion.70
  (167 shorter events, 50.8 us)
Async XLA Ops:
  7.9 299.7 %all-to-all-start = ((bf16[32,256,8]{1,2,0:T(8,128)(2,1)}), bf16[32,256,8]{1,2,0:T(8,128)(2,1)S(1)}, u32[]{:S(2)}, u32[]{:S(2)}) async-start(bf16[32,256,8]{1,2,0:T(8,128)(2,1)} %broadcast_in_dim.201), calls=%async_computation | async-start | bytes 262144 | tf_op jit(solution)/shard_map/all_to_all | solution.py:24
  20.4 280.5 %all-reduce.10.cloned.1.call-start = ((), (), s32[]{:S(2)}) async-start(), calls=%async_computation.3 | async-start | bytes 2097152 | tf_op jit(solution)/shard_map/psum | solution.py:99
  29.1 3.9 copy-start
  32.9 2.1 copy-start.4
  37.2 66.5 %copy-start.16 = (s32[1,1,16]{2,1,0:T(1,128)S(1)}, s32[1,1,16]{2,1,0:T(1,128)}, u32[]{:S(2)}) copy-start(s32[1,1,16]{2,1,0:T(1,128)} %param.15) | copy-start | bytes 196
  37.2 407.6 %all-reduce.6.cloned.1.call-start = ((), (), s32[]{:S(2)}) async-start(), calls=%async_computation.1 | async-start | bytes 786432 | tf_op jit(solution)/shard_map/psum | solution.py:36
  101.0 1.3 copy-start.19
  102.4 18.2 %copy-start.10 = (s32[3]{0:T(128)}, s32[3]{0:T(128)S(1)}, u32[]{:S(2)}) copy-start(s32[3]{0:T(128)S(1)} %compare_select_fusion.5) | copy-start | bytes 40
  103.7 16.9 %copy-start.14 = (pred[3]{0:T(512)(128)(4,1)}, pred[3]{0:T(512)(128)(4,1)S(1)}, u32[]{:S(2)}) copy-start(pred[3]{0:T(512)(128)(4,1)S(1)} %gather_fusion.8) | copy-start | bytes 13
  119.8 0.8 copy-start.21
  122.1 23.4 %copy-start.9 = (bf16[16,256]{1,0:T(8,128)(2,1)S(1)}, bf16[16,256]{1,0:T(8,128)(2,1)}, u32[]{:S(2)}) copy-start(bf16[16,256]{1,0:T(8,128)(2,1)} %param.19) | copy-start | bytes 24580
  300.8 1.9 copy-start.6
  306.9 0.7 copy-start.20
  349.8 2.0 copy-start.1
  349.8 2.0 copy-start.12
  349.8 2.0 copy-start.13
  368.6 1.3 copy-start.3
  370.0 2.9 copy-start.15
  372.3 1.9 copy-start.18
  372.3 3.8 copy-start.22
  374.0 204.1 %copy-start.17 = (pred[16]{0:T(512)(128)(4,1)S(1)}, pred[16]{0:T(512)(128)(4,1)}, u32[]{:S(2)}) copy-start(pred[16]{0:T(512)(128)(4,1)} %get-tuple-element.226) | copy-start | bytes 52
  374.1 216.8 %copy-start.11 = (s32[3]{0:T(128)S(1)}, s32[3]{0:T(128)}, u32[]{:S(2)}) copy-start(s32[3]{0:T(128)} %copy-done.10) | copy-start | bytes 40
  374.1 196.8 %all-reduce.8.cloned.1.call-start = ((), (), s32[]{:S(2)}) async-start(), calls=%async_computation.2 | async-start | bytes 786432 | tf_op jit(solution)/shard_map/psum | solution.py:36
  445.5 148.0 %copy-start.8 = (s32[3]{0:T(128)S(1)}, s32[3]{0:T(128)}, u32[]{:S(2)}) copy-start(s32[3]{0:T(128)} %constant.175.clone.1) | copy-start | bytes 40
  448.5 144.2 %collective-permute-start.1 = (bf16[4,256,256]{2,1,0:T(8,128)(2,1)}, bf16[4,256,256]{2,1,0:T(8,128)(2,1)S(1)}, u32[]{:S(2)}, u32[]{:S(2)}) collective-permute-start(bf16[4,256,256]{2,1,0:T(8,128)(2,1)} %gather_fusion.13), channel_id=1, source_target_pairs={{0,256},{256,0},{32,288},{288,32},{64,320},{320,64},{96,352},{352,... | collective-permute-start | bytes 1572872 | tf_op jit(solution)/shard_map/ppermute | solution.py:47
  573.2 20.3 %collective-permute-start.2 = (bf16[4,256,256]{2,1,0:T(8,128)(2,1)}, bf16[4,256,256]{2,1,0:T(8,128)(2,1)}, u32[]{:S(2)}, u32[]{:S(2)}) collective-permute-start(bf16[4,256,256]{2,1,0:T(8,128)(2,1)} %gather_fusion.15), channel_id=1, source_target_pairs={{0,256},{256,0},{32,288},{288,32},{64,320},{320,64},{96,352},{352,... | collective-permute-start | bytes 1572872 | tf_op jit(solution)/shard_map/ppermute | solution.py:47
  581.0 11.5 %collective-permute-start = (s32[]{:T(128)}, s32[]{:T(128)}, u32[]{:S(2)}, u32[]{:S(2)}) collective-permute-start(s32[]{:T(128)} %select_n.307), channel_id=1, source_target_pairs={{0,256},{256,0},{32,288},{288,32},{64,320},{320,64},{96,352},{352,... | collective-permute-start | bytes 20 | tf_op jit(solution)/shard_map/ppermute | solution.py:47
  585.8 7.0 %collective-permute-start.3 = (s32[4]{0:T(128)S(1)}, s32[4]{0:T(128)S(1)}, u32[]{:S(2)}, u32[]{:S(2)}) collective-permute-start(s32[4]{0:T(128)S(1)} %gather_fusion.16), channel_id=1, source_target_pairs={{0,256},{256,0},{32,288},{288,32},{64,320},{320,64},{96,352},{352,... | collective-permute-start | bytes 56 | tf_op jit(solution)/shard_map/ppermute | solution.py:47
  592.5 29.5 %copy-start.7 = (s32[3]{0:T(128)S(1)}, s32[3]{0:T(128)}, u32[]{:S(2)}) copy-start(s32[3]{0:T(128)} %constant.168.clone.1) | copy-start | bytes 40
  592.7 0.8 copy-start.5
  600.1 74.1 %collective-permute-start.4 = (bf16[4,256,256]{2,1,0:T(8,128)(2,1)S(1)}, bf16[4,256,256]{2,1,0:T(8,128)(2,1)}, u32[]{:S(2)}, u32[]{:S(2)}) collective-permute-start(bf16[4,256,256]{2,1,0:T(8,128)(2,1)S(1)} %get-tuple-element.124), channel_id=1, source_target_pairs={{0,256},{256,0},{32,288},{288,32},{64,320},{320,64},{96,352},{352,... | collective-permute-start | bytes 1572872 | tf_op jit(solution)/shard_map/ppermute | solution.py:47
  676.2 1.3 copy-start.2
Sparse Core Ops, SparseCore 0:
  37.3 263.4 all-reduce.9
  374.2 70.6 all-reduce.5
  447.8 123.0 all-reduce.7
where the time goes:
time: 686 us; the launch traced here: 684 us
  waiting for transfers between devices  295 us (43%)
  blocking collectives  125 us (18%)
  local copies, waits for them, and re-layouts  112 us (16%)
  starting transfers between devices  53 us (8%)
  loops' own time  31.5 us (5%)
  other arithmetic  30.9 us (5%)
  matrix products  19.7 us (3%)
  between operations  17.1 us (2%)
    psum x2, waiting for transfers between devices, spread(): shard = lax.psum(shard, axis)  186 us
    psum x1, waiting for transfers between devices, body(): lax.psum(new_part.astype(jnp.bfloat16), 'prow').astype(jnp.float32)  108 us
    psum x1, blocking collectives, body(): lax.psum(id_part.astype(jnp.bfloat16), 'prow').astype(jnp.float32)  61.9 us
    all_gather x1, blocking collectives, body(): upper_inv = lax.all_gather(u_inverse, 'prow', axis=0, tiled=True)  46.9 us
    gather x2, local copies, waits for them, and re-layouts, pick_rows(): return tile[rows]  40.7 us
    ppermute x5, starting transfers between devices, from_partner(): return lax.ppermute(block, axis, route)  40.3 us
    another operation x1, loops' own time, body(): result = lax.fori_loop(0, (needed + 1) // 2, even_step, result)  28.3 us
    gather x1, local copies, waits for them, and re-layouts, body(): anchor = anchor_top[row_index]  23 us
  transfers between devices with their start and end apart: 9, of which 4 were waited for; matrix products, arithmetic and copies ran while one was open for 13% of the time, Pallas kernels for 0%

commit v1 on v0

--- a/solution.py
+++ b/solution.py
@@ -11,6 +11,7 @@
 UPPER_MOST = 3
 HALF_WORK = 4
 PCOL = ("pcol_0", "pcol_1")
+switch_area = lambda vals: lax.all_gather(vals, axis_name="prow").sum(axis=0)
 
 
 def laid_out(parts, dim):
@@ -96,7 +97,7 @@
     )
     id_part = jnp.where(list_valid & (my_row == 0), listed + 1, 0).astype(jnp.float32)
     new_sum, old_sum, flag_sum, id_sum = (
-        lax.psum(new_part.astype(jnp.bfloat16), "prow").astype(jnp.float32),
+        switch_area(new_part.astype(jnp.bfloat16)).astype(jnp.float32),
         lax.psum(old_part.astype(jnp.bfloat16), "prow").astype(jnp.float32),
         lax.psum(flag_part.astype(jnp.bfloat16), "prow").astype(jnp.float32),
         lax.psum(id_part.astype(jnp.bfloat16), "prow").astype(jnp.float32),

time: 686 us -> 785 us (1.14)
  waiting for transfers between devices: 295 us -> 387 us
  other arithmetic: 30.9 us -> 39.4 us
    all_gather x0 -> x1, waiting for transfers between devices: none -> 139 us  [lax.all_gather(vals, axis_name='prow').sum(axis=0)]
    psum x1, waiting for transfers between devices: 108 us -> 77.1 us  [body(): lax.psum(old_part.astype(jnp.bfloat16), 'prow').astype(jnp.float32)]
    psum x2, waiting for transfers between devices: 186 us -> 171 us  [spread(): shard = lax.psum(shard, axis)]
  transfers between devices with their start and end apart: 9 -> 10, of which waited for: 4 -> 4; matrix products, arithmetic and copies ran while one was open for 13% -> 16% of each run, Pallas kernels for 0% -> 0%
where the time goes in v1:
time: 785 us; the launch traced here: 784 us
  waiting for transfers between devices  387 us (49%)
  blocking collectives  123 us (16%)
  local copies, waits for them, and re-layouts  109 us (14%)
  starting transfers between devices  55.8 us (7%)
  other arithmetic  39.4 us (5%)
  loops' own time  31.8 us (4%)
  matrix products  19.5 us (2%)
  between operations  18 us (2%)
    psum x2, waiting for transfers between devices, spread(): shard = lax.psum(shard, axis)  171 us
    all_gather x1, waiting for transfers between devices, lax.all_gather(vals, axis_name='prow').sum(axis=0)  139 us
    psum x1, waiting for transfers between devices, body(): lax.psum(old_part.astype(jnp.bfloat16), 'prow').astype(jnp.float32)  77.1 us
    psum x1, blocking collectives, body(): lax.psum(id_part.astype(jnp.bfloat16), 'prow').astype(jnp.float32)  60.1 us
    all_gather x1, blocking collectives, body(): upper_inv = lax.all_gather(u_inverse, 'prow', axis=0, tiled=True)  48.4 us
    ppermute x5, starting transfers between devices, from_partner(): return lax.ppermute(block, axis, route)  43.2 us
    gather x2, local copies, waits for them, and re-layouts, pick_rows(): return tile[rows]  40.7 us
    another operation x1, loops' own time, body(): result = lax.fori_loop(0, (needed + 1) // 2, even_step, result)  28.8 us
  transfers between devices with their start and end apart: 10, of which 4 were waited for; matrix products, arithmetic and copies ran while one was open for 16% of the time, Pallas kernels for 0%

profile of v1, /device:TPU:484, one launch (start us, length us, event | category | flops | bytes accessed | tf_op | source)
XLA Modules:
  0.0 783.9 jit_solution(6393618883489537406)
XLA Ops:
  11.3 3.8 convolution_convert_fusion.2
  15.1 2.5 copy.127
  17.6 2.3 gather_fusion.2
  25.5 12.5 %all-to-all-start = ((bf16[32,256,8]{1,2,0:T(8,128)(2,1)}), bf16[32,256,8]{1,2,0:T(8,128)(2,1)S(1)}, u32[]{:S(2)}, u32[]{:S(2)}) async-start(bf16[32,256,8]{1,2,0:T(8,128)(2,1)} %broadcast_in_dim.201), calls=%async_computation | async-start | bytes 262144 | tf_op jit(solution)/shard_map/all_to_all | solution.py:25
  38.1 6.4 psum.52
  44.6 60.1 %all-reduce = (bf16[4]{0:T(256)(128)(2,1)S(1)}, bf16[8]{0:T(256)(128)(2,1)S(1)}) all-reduce(bf16[4]{0:T(256)(128)(2,1)S(1)} %get-tuple-element.279, bf16[8]{0:T(256)(128)(2,1)S(1)} %multiply_reduce_fusion), channel_id=1, replica_groups=mesh['prow'=16,'pcol_0'=4,'pcol_1'=8] {'prow'}, use_global_device_ids=true, to_apply=%region_6.7 | all-reduce | flops 12 | bytes 48 | tf_op jit(solution)/shard_map/psum | solution.py:103
  104.7 8.3 %psum.53 = s32[3]{0:T(128)S(1)} all-reduce(s32[3]{0:T(128)S(1)} %psum.52), channel_id=1, replica_groups=mesh['prow'=16,'pcol_0'=4,'pcol_1'=8] {'pcol_1'}, use_global_device_ids=true, to_apply=%region_14.15 | all-reduce | flops 3 | bytes 24 | tf_op jit(solution)/shard_map/psum | solution.py:37
  117.0 23.0 %gather_fusion.6 = s32[4096]{0:T(1024)S(1)} fusion(s32[65536]{0:T(1024)S(1)} %scatter_custom_fusion, s32[4096]{0:T(1024)S(1)} %broadcast_clamp_fusion), kind=kCustom, calls=%fused_computation.6 | custom fusion | bytes 49152 | tf_op jit(solution)/shard_map/gather | solution.py:121
  140.9 48.4 %all_gather.11 = bf16[256,256]{1,0:T(8,128)(2,1)} all-gather(bf16[16,256]{1,0:T(8,128)(2,1)S(1)} %copy-done.8), channel_id=1, replica_groups=mesh['prow'=16,'pcol_0'=4,'pcol_1'=8] {'prow'}, dimensions={0}, use_global_device_ids=true | all-gather | bytes 139264 | tf_op jit(solution)/shard_map/all_gather | solution.py:71
  190.6 77.1 %all-reduce.5.cloned.1.call-done = bf16[4,256,256]{2,0,1:T(4,128)(2,1)} async-done(((bf16[4,256,256]{2,0,1:T(4,128)(2,1)}), bf16[4,256,256]{2,0,1:T(4,128)(2,1)}) %all-reduce.5.cloned.1.call-update) | async-done | bytes 524304 | tf_op jit(solution)/shard_map/psum | solution.py:101
  270.2 40.7 %gather_fusion.18 = bf16[4096,256]{1,0:T(8,128)(2,1)} fusion(bf16[16,256,256]{2,1,0:T(8,128)(2,1)S(1)} %gather_fusion.7, s32[4096]{0:T(1024)S(1)} %bitcast.154), kind=kCustom, calls=%fused_computation.18 | custom fusion | bytes 4227072 | tf_op jit(solution)/shard_map/vmap()/gather | solution.py:52
  310.9 139.2 %all-gather.3.cloned.1.call-done = bf16[64,256,256]{2,1,0:T(8,128)(2,1)} async-done(((bf16[4,256,256]{2,1,0:T(8,128)(2,1)}), bf16[64,256,256]{2,1,0:T(8,128)(2,1)}) %all-gather.3.cloned.1.call-update) | async-done | bytes 8388624 | tf_op jit(solution)/shard_map/all_gather | solution.py:14
  450.1 5.0 reduce_sum.51
  456.6 2.0 gather_fusion.5
  459.1 2.3 gather_fusion.4
  461.4 16.0 %copy_select_fusion = (bf16[16,256,256]{2,0,1:T(8,128)(2,1)}, bf16[16,256,256]{2,0,1:T(8,128)(2,1)S(1)}) fusion(bf16[16,256,256]{2,1,0:T(8,128)(2,1)} %gather_fusion.4, pred[16]{0:T(512)(128)(4,1)S(1)} %iota_compare_fusion.3, pred[16]{0:T(512)(128)(4,1)S(1)} %copy-done.14, bf16[1,1,16,256,256]{4,3,2,1,0:T(8,128)(2,1)S(1)} %copy-done.1, ...), kind=kLoop, calls=%fused_computation.46 | loop fusion | flops 4194304 | bytes 12587056 | tf_op jit(solution)/shard_map/jit(_where)/select_n | solution.py:155
  479.5 2.3 copy.103
  485.8 53.6 %all-reduce.7.cloned.1.call-done = bf16[3,256,256]{2,1,0:T(8,128)(2,1)} async-done(((bf16[3,256,256]{2,1,0:T(8,128)(2,1)}), bf16[3,256,256]{2,1,0:T(8,128)(2,1)}) %all-reduce.7.cloned.1.call-update) | async-done | bytes 393232 | tf_op jit(solution)/shard_map/psum | solution.py:37
  540.7 2.2 gather_fusion.13
  542.9 4.9 collective-permute-start.1
  547.8 117.4 %all-reduce.9.cloned.1.call-done = bf16[3,256,256]{2,1,0:T(8,128)(2,1)} async-done(((bf16[3,256,256]{2,1,0:T(8,128)(2,1)}), bf16[3,256,256]{2,1,0:T(8,128)(2,1)}) %all-reduce.9.cloned.1.call-update) | async-done | bytes 393232 | tf_op jit(solution)/shard_map/psum | solution.py:37
  665.2 2.5 gather_fusion.15
  667.7 4.9 collective-permute-start.2
  676.7 3.7 collective-permute-start
  681.6 4.9 collective-permute-start.3
  689.7 7.5 while.23
  697.2 24.7 %collective-permute-start.4 = (bf16[4,256,256]{2,1,0:T(8,128)(2,1)S(1)}, bf16[4,256,256]{2,1,0:T(8,128)(2,1)}, u32[]{:S(2)}, u32[]{:S(2)}) collective-permute-start(bf16[4,256,256]{2,1,0:T(8,128)(2,1)S(1)} %get-tuple-element.124), channel_id=1, source_target_pairs={{0,256},{256,0},{32,288},{288,32},{64,320},{320,64},{96,352},{352,... | collective-permute-start | bytes 1572872 | tf_op jit(solution)/shard_map/ppermute | solution.py:48
  721.9 51.5 %while.22 = (s32[]{:T(128)}, bf16[16,256,256]{2,1,0:T(8,128)(2,1)S(1)}, s32[]{:T(128)}, s32[16]{0:T(128)S(1)}, bf16[16,256,256]{2,1,0:T(8,128)(2,1)}, /*index=5*...) while((s32[]{:T(128)}, ...), condition=%wide.region_24.25_spmd, body=%wide.region_22.24_spmd.sunk | while | flops 33816608 | bytes 656746 | solution.py:189
  730.4 1.8 fusion.70
  740.7 1.8 fusion.70
  761.3 1.8 fusion.70
  771.6 1.8 fusion.70
  (170 shorter events, 56.0 us)
Async XLA Ops:
  6.5 8.6 %copy-start = (bf16[1,1,16,256,256]{4,3,2,1,0:T(8,128)(2,1)S(1)}, bf16[1,1,16,256,256]{4,3,2,1,0:T(8,128)(2,1)}, u32[]{:S(2)}) copy-start(bf16[1,1,16,256,256]{4,3,2,1,0:T(8,128)(2,1)} %param.14) | copy-start | bytes 6291460
  6.5 261.1 %all-reduce.5.cloned.1.call-start = ((), (), s32[]{:S(2)}) async-start(), calls=%async_computation.1 | async-start | bytes 1048576 | tf_op jit(solution)/shard_map/psum | solution.py:101
  15.1 435.1 %all-gather.3.cloned.1.call-start = ((), (), s32[]{:S(2)}) async-start(), calls=%async_computation.4 | async-start | bytes 8912896 | tf_op jit(solution)/shard_map/all_gather | solution.py:14
  21.3 3.5 copy-start.9
  23.6 91.8 %copy-start.10 = (s32[3]{0:T(128)}, s32[3]{0:T(128)S(1)}, u32[]{:S(2)}) copy-start(s32[3]{0:T(128)S(1)} %compare_select_fusion.5) | copy-start | bytes 40
  24.8 90.5 %copy-start.15 = (pred[3]{0:T(512)(128)(4,1)}, pred[3]{0:T(512)(128)(4,1)S(1)}, u32[]{:S(2)}) copy-start(pred[3]{0:T(512)(128)(4,1)S(1)} %gather_fusion.8) | copy-start | bytes 13
  25.5 433.1 %all-to-all-start = ((bf16[32,256,8]{1,2,0:T(8,128)(2,1)}), bf16[32,256,8]{1,2,0:T(8,128)(2,1)S(1)}, u32[]{:S(2)}, u32[]{:S(2)}) async-start(bf16[32,256,8]{1,2,0:T(8,128)(2,1)} %broadcast_in_dim.201), calls=%async_computation | async-start | bytes 262144 | tf_op jit(solution)/shard_map/all_to_all | solution.py:25
  38.0 501.4 %all-reduce.7.cloned.1.call-start = ((), (), s32[]{:S(2)}) async-start(), calls=%async_computation.2 | async-start | bytes 786432 | tf_op jit(solution)/shard_map/psum | solution.py:37
  112.9 4.0 copy-start.20
  116.9 23.9 %copy-start.8 = (bf16[16,256]{1,0:T(8,128)(2,1)S(1)}, bf16[16,256]{1,0:T(8,128)(2,1)}, u32[]{:S(2)}) copy-start(bf16[16,256]{1,0:T(8,128)(2,1)} %param.19) | copy-start | bytes 24580
  116.9 73.6 %copy-start.17 = (s32[1,1,16]{2,1,0:T(1,128)S(1)}, s32[1,1,16]{2,1,0:T(1,128)}, u32[]{:S(2)}) copy-start(s32[1,1,16]{2,1,0:T(1,128)} %param.15) | copy-start | bytes 196
  459.1 2.3 copy-start.1
  459.1 2.3 copy-start.4
  459.1 2.3 copy-start.13
  459.1 2.3 copy-start.14
  478.2 1.3 copy-start.3
  479.5 3.0 copy-start.5
  479.5 3.0 copy-start.16
  481.8 1.9 copy-start.18
  481.8 1.9 copy-start.19
  481.9 3.8 copy-start.21
  483.6 181.6 %all-reduce.9.cloned.1.call-start = ((), (), s32[]{:S(2)}) async-start(), calls=%async_computation.3 | async-start | bytes 786432 | tf_op jit(solution)/shard_map/psum | solution.py:37
  485.8 54.3 %copy-start.11 = (s32[4]{0:T(128)}, s32[4]{0:T(128)S(1)}, u32[]{:S(2)}) copy-start(s32[4]{0:T(128)S(1)} %fusion.48) | copy-start | bytes 52
  539.4 148.4 %copy-start.7 = (s32[1024]{0:T(1024)}, s32[1024]{0:T(1024)S(1)}, u32[]{:S(2)}) copy-start(s32[1024]{0:T(1024)S(1)} %pad_clamp_fusion.1) | copy-start | bytes 12292
  542.9 146.8 %collective-permute-start.1 = (bf16[4,256,256]{2,1,0:T(8,128)(2,1)S(1)}, bf16[4,256,256]{2,1,0:T(8,128)(2,1)S(1)}, u32[]{:S(2)}, u32[]{:S(2)}) collective-permute-start(bf16[4,256,256]{2,1,0:T(8,128)(2,1)S(1)} %gather_fusion.13), channel_id=1, source_target_pairs={{0,256},{256,0},{32,288},{288,32},{64,320},{320,64},{96,352},{352,... | collective-permute-start | bytes 1572872 | tf_op jit(solution)/shard_map/ppermute | solution.py:48
  667.7 21.9 %collective-permute-start.2 = (bf16[4,256,256]{2,1,0:T(8,128)(2,1)}, bf16[4,256,256]{2,1,0:T(8,128)(2,1)}, u32[]{:S(2)}, u32[]{:S(2)}) collective-permute-start(bf16[4,256,256]{2,1,0:T(8,128)(2,1)} %gather_fusion.15), channel_id=1, source_target_pairs={{0,256},{256,0},{32,288},{288,32},{64,320},{320,64},{96,352},{352,... | collective-permute-start | bytes 1572872 | tf_op jit(solution)/shard_map/ppermute | solution.py:48
  676.7 12.9 %collective-permute-start = (s32[]{:T(128)}, s32[]{:T(128)}, u32[]{:S(2)}, u32[]{:S(2)}) collective-permute-start(s32[]{:T(128)} %select_n.307), channel_id=1, source_target_pairs={{0,256},{256,0},{32,288},{288,32},{64,320},{320,64},{96,352},{352,... | collective-permute-start | bytes 20 | tf_op jit(solution)/shard_map/ppermute | solution.py:48
  681.6 8.0 %collective-permute-start.3 = (s32[4]{0:T(128)}, s32[4]{0:T(128)}, u32[]{:S(2)}, u32[]{:S(2)}) collective-permute-start(s32[4]{0:T(128)} %gather_fusion.16), channel_id=1, source_target_pairs={{0,256},{256,0},{32,288},{288,32},{64,320},{320,64},{96,352},{352,... | collective-permute-start | bytes 56 | tf_op jit(solution)/shard_map/ppermute | solution.py:48
  689.6 32.3 %copy-start.6 = (s32[3]{0:T(128)S(1)}, s32[3]{0:T(128)}, u32[]{:S(2)}) copy-start(s32[3]{0:T(128)} %constant.169.clone.1) | copy-start | bytes 40
  697.2 77.0 %collective-permute-start.4 = (bf16[4,256,256]{2,1,0:T(8,128)(2,1)S(1)}, bf16[4,256,256]{2,1,0:T(8,128)(2,1)}, u32[]{:S(2)}, u32[]{:S(2)}) collective-permute-start(bf16[4,256,256]{2,1,0:T(8,128)(2,1)S(1)} %get-tuple-element.124), channel_id=1, source_target_pairs={{0,256},{256,0},{32,288},{288,32},{64,320},{320,64},{96,352},{352,... | collective-permute-start | bytes 1572872 | tf_op jit(solution)/shard_map/ppermute | solution.py:48
  773.4 1.9 copy-start.12
  776.0 1.3 copy-start.2
Sparse Core Ops, SparseCore 0:
  15.2 252.4 all-reduce.4
  270.9 179.1 all-gather.2
  483.8 55.5 all-reduce.6
  542.2 123.0 all-reduce.8
